TPU v7x, 128 devices: a whole 4x4x4 slice. The times are simulated.
128 devices in a mesh: grp: 4 (over y), row: 32 (over z, x, core).
Axes of the slice: x: 4, y: 4, z: 4, core: 2. Of those that a mesh axis runs over, the one named last changes fastest.
Arguments:
- tiles: bfloat16 [4, 32, 32, 256, 256], P('grp', 'row'), may hold values from -0.046875 to 0.046875
- tile_rows: int32 [4, 32, 32], P('grp', 'row'), may hold values from 0 to 3, as said below
- tile_cols: int32 [4, 32, 32], P('grp', 'row'), may hold values from 0 to 31, as said below
- live_tiles: int32 [4, 32], P('grp', 'row'), may hold values from 16 to 32, as said below
- dual_shift: float32 [32768], P('row'), may hold values from 0.5 to 2
- start_block: float32 [32, 32768], P(None, 'row'), may hold values from -6 to 6
Outputs:
- projections: float32 [4, 32, 128], replicated
- factors: float32 [4, 32, 32], replicated
- next_block: float32 [32, 32768], P(None, 'row')
Inputs may be any that keep to these rules, and one draw needn't show every extreme that they name: `tile_rows`: the tile slots of one device sit at distinct positions (block row, column block), padding slots included. `tile_cols`: column block j of group g is global block column (j // 1) * 4 + g * 1 + j % 1. Slots from live_tiles on are padding with arbitrary values; in every draw some device has all 32 slots live.
All inputs are finite; a program needn't handle non-finite values.
Results may differ from a plain program's by a relative error of at most 0.013.
Values may be sent and summed in bfloat16 or wider, within the bound.
A program may use at most 64 MiB of HBM per device.

v0:
```python
import contextlib
import functools

import jax
import jax.numpy as jnp
from jax import lax
from jax.experimental import pallas as pl
from jax.experimental.pallas import tpu as pltpu
from jax.sharding import PartitionSpec as P

MESH = pl.DeviceIdType.MESH
HIGHEST = lax.Precision.HIGHEST
F32 = jnp.float32
BF16 = jnp.bfloat16

ITERS = 4
K = 32
BS = 256
GRP = 4
ROW = 32
CHIPS = ROW // 2
SIDE = 4
TILES = 32
WAVES = (5, 5, 3, 2)
PARTS = 4
SHIFT = -1.0

FAR_FIRST = sorted(
    [(dz, dx) for dz in range(SIDE) for dx in range(SIDE) if (dz, dx) != (0, 0)],
    key=lambda d: -(min(d[0], SIDE - d[0]) + min(d[1], SIDE - d[1])),
)
SMALL_GROUP = [(dy, dc) for dy in (2, 1, 3, 0) for dc in (1, 0) if (dy, dc) != (0, 0)]


def height(step):
    return 2 * K if step == 0 else K


@contextlib.contextmanager
def phase(name):
    with jax.named_scope(name):
        yield
    if name in ("update", "cholesky", "dots", "direct", "pairs"):
        pl.delay(1)


def wave_of(m):
    return next(w for w in range(len(WAVES)) if m < sum(WAVES[: w + 1]))


def dots_height(step):
    return K if step < ITERS else K + 8


def dot(left, right, precision=None):
    return lax.dot_general(
        left, right, (((1,), (0,)), ((), ())), precision=precision, preferred_element_type=F32
    )


def t_dot(left, right, precision=None):
    return lax.dot_general(
        left, right, (((0,), (0,)), ((), ())), precision=precision, preferred_element_type=F32
    )


def dot_t(left, right, precision=None):
    return lax.dot_general(
        left, right, (((1,), (1,)), ((), ())), precision=precision, preferred_element_type=F32
    )


def cholesky(gram):
    row = lax.broadcasted_iota(jnp.int32, (K, K), 0)
    col = lax.broadcasted_iota(jnp.int32, (K, K), 1)
    left = gram
    right = jnp.where(row == col, 1.0, 0.0).astype(F32)
    for k in range(0, K - 2, 2):
        first = jnp.broadcast_to(left[:, k : k + 1], (K, K))
        second = jnp.broadcast_to(left[:, k + 1 : k + 2], (K, K))
        a = first[k : k + 1, :]
        b = second[k : k + 1, :]
        d = second[k + 1 : k + 2, :]
        inverse = 1.0 / (a * d - b * b)
        below = row > k + 1
        of_first = jnp.where(below, first * (d * inverse) - second * (b * inverse), 0.0)
        of_second = jnp.where(below, second * (a * inverse) - first * (b * inverse), 0.0)
        left_k, left_l = left[k : k + 1, :], left[k + 1 : k + 2, :]
        right_k, right_l = right[k : k + 1, :], right[k + 1 : k + 2, :]
        left = left - of_first * left_k - of_second * left_l
        right = right - of_first * right_k - of_second * right_l
    odd = (row & 1) == 1
    pivots = jnp.sum(jnp.where(row == col, left, 0.0), axis=1, keepdims=True)
    beside = jnp.sum(jnp.where(row + 1 == col, left, 0.0), axis=1, keepdims=True)
    factor = jnp.where(odd, pltpu.roll(jnp.broadcast_to(beside / pivots, (K, K)), 1, 0), 0.0)
    left = left - factor * pltpu.roll(left, 1, 0)
    right = right - factor * pltpu.roll(right, 1, 0)
    pivots = jnp.sum(jnp.where(row == col, left, 0.0), axis=1, keepdims=True)
    scale = 1.0 / jnp.sqrt(pivots)
    return jnp.where(col >= row, left * scale, 0.0), jnp.where(col <= row, right * scale, 0.0)


def kernel(
    rows_hbm,
    cols_hbm,
    live_hbm,
    tiles_hbm,
    start_hbm,
    dual_hbm,
    proj_ref,
    fact_ref,
    next_ref,
    rows_smem,
    cols_smem,
    live_smem,
    dual_ref,
    gram_ref,
    start_gram,
    start_grams,
    slot_vmem,
    slot_ref,
    start_ref,
    tiles,
    turned,
    cols_0,
    cols_1,
    cols_2,
    cols_3,
    rows_0,
    rows_1,
    rows_2,
    rows_3,
    raw_x,
    basis,
    in_blocks,
    old_rows,
    trans,
    products,
    pair_out,
    pair_in,
    back_out,
    back_in,
    own_back,
    own_direct,
    direct_out,
    direct_in,
    dots,
    last,
    load_sem,
    slot_sem,
    tile_sem,
    pair_gram_send,
    pair_gram_recv,
    gram_send,
    gram_recv,
    last_send,
    last_recv,
    cols_send,
    cols_recv,
    relay_send,
    relay_recv,
    rows_send,
    rows_recv,
    raw_send,
    raw_recv,
    dots_send,
    dots_recv,
    pair_send,
    pair_recv,
    back_send,
    back_recv,
    direct_send,
    direct_recv,
):
    cols_x = (cols_0, cols_1, cols_2, cols_3)
    rows_x = (rows_0, rows_1, rows_2, rows_3)
    g = lax.axis_index("grp")
    r = lax.axis_index("row")
    core = lax.rem(r, 2)
    chip = lax.div(r, 2)
    z = lax.div(chip, SIDE)
    x = lax.rem(chip, SIDE)
    partner = r + 1 - 2 * core

    def chip_at(dz, dx):
        return lax.rem(z + dz, SIDE) * SIDE + lax.rem(x + dx, SIDE)

    def chip_from(dz, dx):
        return lax.rem(z + SIDE - dz, SIDE) * SIDE + lax.rem(x + SIDE - dx, SIDE)

    def remote(src, dst, send, recv, group, owner):
        return pltpu.make_async_remote_copy(
            src_ref=src,
            dst_ref=dst,
            send_sem=send,
            recv_sem=recv,
            device_id=(group, owner),
            device_id_type=MESH,
        )

    def await_recv(ref, send, recv):
        remote(ref, ref, send, recv, g, partner).wait_recv()

    def await_send(ref, send, recv):
        remote(ref, ref, send, recv, g, partner).wait_send()

    barrier = pltpu.get_barrier_semaphore()
    for dz, dx in FAR_FIRST:
        pl.semaphore_signal(
            barrier, inc=1, device_id=(g, chip_at(dz, dx) * 2 + core), device_id_type=MESH
        )
    for dy, dc in SMALL_GROUP:
        pl.semaphore_signal(
            barrier,
            inc=1,
            device_id=(lax.rem(g + dy, GRP), partner if dc else r),
            device_id_type=MESH,
        )

    loads = [
        pltpu.make_async_copy(src, dst, load_sem.at[i])
        for i, (src, dst) in enumerate(
            [
                (rows_hbm, rows_smem),
                (cols_hbm, cols_smem),
                (live_hbm, live_smem),
                (start_hbm, start_ref),
                (dual_hbm, dual_ref),
            ]
        )
    ]
    for copy in loads:
        copy.start()
    load = pltpu.make_async_copy(tiles_hbm, tiles, tile_sem)
    load.start()

    trans[...] = jnp.zeros_like(trans)
    products[TILES] = jnp.zeros((K, BS), F32)
    proj_ref[...] = jnp.zeros_like(proj_ref)
    for copy in loads:
        copy.wait()

    lane = lax.broadcasted_iota(jnp.int32, (1, GRP * ROW), 1)
    slots = jnp.full((1, GRP * ROW), TILES, jnp.int32)
    for k in range(TILES):
        place = jnp.where(live_smem[0, 0] > k, rows_smem[0, 0, k] * ROW + cols_smem[0, 0, k], -1)
        slots = jnp.where(lane == place, k, slots)
    slot_vmem[...] = slots
    table = pltpu.make_async_copy(slot_vmem, slot_ref, slot_sem)
    table.start()

    for i in range(GRP):
        block = start_ref[:, i * BS : (i + 1) * BS]
        high = block.astype(BF16)
        rows_0[i, 0:K, :] = high
        rows_0[i, K : 2 * K, :] = (block - high.astype(F32)).astype(BF16)
        raw_x[i, 0:K, :] = block
    cols_0[r] = rows_0[g]
    gram = dot_t(start_ref[...], start_ref[...], HIGHEST)
    for i in range(4):
        start_gram[core, :, i * K : (i + 1) * K] = gram[8 * i : 8 * i + 8]
    dual = dual_ref[:, pl.ds(pl.multiple_of(g * BS, BS), BS)]

    def send_cols(step):
        here = cols_x[step].at[r]
        for m, (dz, dx) in enumerate(FAR_FIRST):
            remote(
                here, here, cols_send, cols_recv.at[step % 2, wave_of(m)], g, chip_at(dz, dx) * 2 + core
            ).start()
        remote(here, here, relay_send, relay_recv.at[step % 2], g, partner).start()

    def receive_cols(step):
        first = 0
        for wave, count in enumerate(WAVES):
            await_recv(
                cols_x[step].at[pl.ds(0, count)], cols_send, cols_recv.at[step % 2, wave]
            )
            for m in range(first, first + count):
                there = cols_x[step].at[chip_from(*FAR_FIRST[m]) * 2 + core]
                remote(there, there, relay_send, relay_recv.at[step % 2], g, partner).start()
            first += count

    def sent(step):
        await_send(cols_x[step].at[pl.ds(0, CHIPS - 1)], cols_send, cols_recv.at[0, 0])
        await_send(cols_x[step].at[pl.ds(0, CHIPS)], relay_send, relay_recv.at[0])
        await_send(pair_out.at[step], pair_send, pair_recv.at[0])
        await_send(back_in.at[step, pl.ds(0, CHIPS - 1)], back_send, back_recv.at[0])
        await_send(direct_in.at[step, pl.ds(0, 3)], direct_send, direct_recv.at[0])
        if step > 0:
            await_send(rows_x[step].at[pl.ds(0, 3)], rows_send, rows_recv.at[0])
            await_send(dots.at[step, pl.ds(0, 7), pl.ds(0, K)], dots_send, dots_recv.at[0])

    def send_raw(step):
        if step > 1:
            receive_raw(step - 1)
        mine = raw_x.at[g, pl.ds(K * step, K), :]
        for dy in (2, 1, 3):
            remote(
                mine, mine, raw_send, raw_recv.at[step % 2], lax.rem(g + dy, GRP), r
            ).start()

    def receive_raw(step):
        others = raw_x.at[pl.ds(0, 3), pl.ds(K * step, K), :]
        await_recv(others, raw_send, raw_recv.at[step % 2])
        await_send(others, raw_send, raw_recv.at[step % 2])

    def products_of(load_left, rows, matrices):
        def body(k, carry):
            product = dot(load_left(k), matrices[k])
            if rows == 2 * K:
                product = product[:K] + product[K:]
            products[k] = product
            return carry

        lax.fori_loop(0, TILES, body, 0, unroll=True)

    def back_sum(owner):
        total = products[slot_ref[0, owner]]
        for i in range(1, GRP):
            total = total + products[slot_ref[0, i * ROW + owner]]
        return total

    def send_pairs(step):
        for part in range(PARTS):

            def other(m, carry):
                pair_out[step, m] = back_sum(m * 2 + 1 - core).astype(BF16)
                return carry

            size = CHIPS // PARTS
            lax.fori_loop(part * size, part * size + size, other, 0, unroll=2)
            here = pl.ds(part * size, size)
            remote(
                pair_out.at[step, here],
                pair_in.at[step, here],
                pair_send,
                pair_recv.at[step % 2],
                g,
                partner,
            ).start()

    def own_sums(step):
        def mine(m, carry):
            own_back[m] = back_sum(m * 2 + core)
            return carry

        lax.fori_loop(0, CHIPS, mine, 0, unroll=2)

    def send_back(step):
        with phase("wait_pair"):
            await_recv(pair_in.at[step], pair_send, pair_recv.at[step % 2])
        for dz, dx in FAR_FIRST:
            there = chip_at(dz, dx)
            back_out[step, there] = (
                own_back[there] + pair_in[step, there].astype(F32)
            ).astype(BF16)
        for dz, dx in FAR_FIRST:
            there = chip_at(dz, dx)
            remote(
                back_out.at[step, there],
                back_in.at[step, chip],
                back_send,
                back_recv.at[step % 2],
                g,
                there * 2 + core,
            ).start()

    def send_direct(step):
        for dy in (2, 1, 3, 0):
            group = lax.rem(g + dy, GRP)

            def add(j, total, group=group):
                return total + products[slot_ref[0, group * ROW + j]]

            total = lax.fori_loop(0, ROW, add, jnp.zeros((K, BS), F32), unroll=8)
            if dy == 0:
                own_direct[...] = total
                continue
            direct_out[step, group] = total.astype(BF16)
            remote(
                direct_out.at[step, group],
                direct_in.at[step, g],
                direct_send,
                direct_recv.at[step % 2],
                group,
                r,
            ).start()

    def send_start_gram():
        await_recv(start_gram.at[0], pair_gram_send, pair_gram_recv)
        start_grams[chip] = start_gram[0] + start_gram[1]
        mine = start_grams.at[chip]
        for dz, dx in FAR_FIRST:
            remote(mine, mine, gram_send, gram_recv, g, chip_at(dz, dx) * 2 + core).start()

    def receive_start_gram():
        await_recv(start_grams.at[pl.ds(0, CHIPS - 1)], gram_send, gram_recv)
        total = start_grams[0]
        for i in range(1, CHIPS):
            total = total + start_grams[i]
        return jnp.concatenate([total[:, i * K : (i + 1) * K] for i in range(4)], axis=0)

    def send_dots(step):
        width = K * step + K

        totals = [jnp.zeros((K, width), F32) for _ in range(4)]
        for p in range(CHIPS):
            owner = p * 2 + core
            so_far = jnp.concatenate([cols_x[s][owner, 0:K] for s in range(step + 1)], axis=0)
            totals[p % 4] = totals[p % 4] + dot_t(cols_x[step][owner], so_far)
        total = (totals[0] + totals[1]) + (totals[2] + totals[3])
        here = g * 2 + core
        dots[step, here, 0:K, 0:width] = total
        spread_dots(step)

    def spread_dots(step):
        here = g * 2 + core
        mine = dots.at[step, here, pl.ds(0, dots_height(step))]
        for dy, dc in SMALL_GROUP:
            remote(
                mine,
                mine,
                dots_send,
                dots_recv.at[step % 2],
                lax.rem(g + dy, GRP),
                partner if dc else r,
            ).start()

    def send_last():
        block = raw_x[g, K * ITERS :, :]
        last[chip, 0:K, :] = dot_t(block, raw_x[g, 0 : K * ITERS, :], HIGHEST)
        gram = dot_t(block, block, HIGHEST)
        for i in range(4):
            last[chip, K:, i * K : (i + 1) * K] = gram[8 * i : 8 * i + 8]
        mine = last.at[chip]
        for dz, dx in FAR_FIRST:
            remote(mine, mine, last_send, last_recv, g, chip_at(dz, dx) * 2 + core).start()

    def spread_last():
        await_recv(last.at[pl.ds(0, CHIPS - 1)], last_send, last_recv)
        total = last[0]
        for i in range(1, CHIPS):
            total = total + last[i]
        dots[ITERS, g * 2 + core] = total
        spread_dots(ITERS)

    def receive_dots(step):
        with phase("wait_dots"):
            await_recv(
                dots.at[step, pl.ds(0, 7), pl.ds(0, dots_height(step))],
                dots_send,
                dots_recv.at[step % 2],
            )
        total = dots[step, 0, 0 : dots_height(step)]
        for i in range(1, 2 * GRP):
            total = total + dots[step, i, 0 : dots_height(step)]
        if step < ITERS:
            gram = total[:, K * step : K + K * step]
        else:
            gram = jnp.concatenate([total[K:, i * K : (i + 1) * K] for i in range(4)], axis=0)
        products_before = total[0:K, : K * step]
        coef = dot_t(products_before, trans[0 : K * step, 0 : K * step], HIGHEST)
        return products_before, coef, gram - dot_t(coef, coef, HIGHEST)

    def scaled(step, coef, gram):
        if step > 1:
            coef = dot(inverses[step - 1], coef, HIGHEST)
            gram = dot_t(dot(inverses[step - 1], gram, HIGHEST), inverses[step - 1], HIGHEST)
        gram_ref[...] = gram
        return coef, gram_ref[...]

    def normalise(step, coef, gram):
        with phase("cholesky"):
            upper, inverse = cholesky(gram)
        if step > 0:
            fact_ref[step - 1] = upper.T
        if step < ITERS:
            own = inverse if step < 2 else dot(inverse, inverses[step - 1], HIGHEST)
            trans[K * step : K + K * step, K * step : K + K * step] = own
            if step > 0:
                trans[K * step : K + K * step, 0 : K * step] = -dot(
                    inverse,
                    dot(coef, trans[0 : K * step, 0 : K * step], HIGHEST),
                    HIGHEST,
                )
        uppers[step] = upper
        inverses[step] = inverse

    def record(step, coef):
        row = lax.broadcasted_iota(jnp.int32, (K, K), 0)
        col = lax.broadcasted_iota(jnp.int32, (K, K), 1)
        at = K * (step - 1)
        if step > 1:
            if step > 2:
                proj_ref[step - 1, :, 0 : at - K] = coef[:, : at - K]
            proj_ref[step - 1, :, at - K : at] = coef[:, at - K : at] + uppers[step - 1]
        proj_ref[step - 1, :, at : at + K] = coef[:, at:] + jnp.where(row == col, SHIFT, 0.0)

    uppers = {}
    inverses = {}
    scope = phase
    ahead = None
    for step in range(ITERS):
        size = height(step)
        if ahead is not None:
            newest = ahead()
        if step == 0:
            with scope("enter"):
                pl.semaphore_wait(barrier, len(FAR_FIRST) + len(SMALL_GROUP))
            mine = start_gram.at[core]
            remote(mine, mine, pair_gram_send, pair_gram_recv, g, partner).start()
            send_cols(0)
            with scope("load"):
                load.wait()
                table.wait()
            with scope("back"):
                products_of(lambda k: rows_0[rows_smem[0, 0, k]], size, tiles)
        else:
            with scope("wait_rows"):
                await_recv(rows_x[step].at[pl.ds(0, 3)], rows_send, rows_recv.at[step % 2])
            send_raw(step)
            with scope("back"):
                products_of(lambda k, step=step: rows_x[step][rows_smem[0, 0, k]], size, tiles)
        with scope("pairs"):
            send_pairs(step)
        with scope("own_sums"):
            own_sums(step)
            if step == 0:
                send_start_gram()
        if step == 0:
            with scope("turn"):

                def turn(k, carry):
                    turned[k] = tiles[k].T
                    return carry

                lax.fori_loop(0, TILES, turn, 0, unroll=2)

        @pl.when(core == 0)
        def _(step=step):
            send_back(step)

        with scope("wait_cols"):
            receive_cols(step)
        if step > 0:
            with scope("dots"):
                send_dots(step)

        @pl.when(core == 1)
        def _(step=step):
            send_back(step)

        with scope("wait_relay"):
            await_recv(cols_x[step].at[pl.ds(0, CHIPS)], relay_send, relay_recv.at[step % 2])
        with scope("forward"):
            products_of(lambda k, step=step: cols_x[step][cols_smem[0, 0, k]], size, turned)
        with scope("direct"):
            send_direct(step)

        if step == 0:
            with scope("wait_dots"):
                coef, gram = None, receive_start_gram()
            normalise(0, None, gram)
            first = dot(inverses[0], raw_x[g, 0:K, :], HIGHEST)
            known = first * (-SHIFT)
            basis[0:K, 0:BS] = first
        else:
            before, coef, gram = receive_dots(step)
            with scope("known"):
                known = raw_x[g, K * step : K * step + K, :] * (-SHIFT)
                known = known - dot(before, in_blocks[0 : K * step, :], HIGHEST)
                known = known - dot(gram, newest, HIGHEST)

        with scope("wait_direct"):
            await_recv(
                direct_in.at[step, pl.ds(0, 3)], direct_send, direct_recv.at[step % 2]
            )
        with scope("wait_back"):
            await_recv(
                back_in.at[step, pl.ds(0, CHIPS - 1)], back_send, back_recv.at[step % 2]
            )
        with scope("update"):
            total = own_direct[...]
            for dy in (1, 2, 3):
                total = total + direct_in[step, lax.rem(g + dy, GRP)].astype(F32)
            total = total + own_back[chip] + pair_in[step, chip].astype(F32)
            for dz, dx in FAR_FIRST:
                total = total + back_in[step, chip_at(dz, dx)].astype(F32)
            image = 0.5 * total - raw_x[g, K * step : K * step + K, :] * dual
            if step == 0:
                image = dot(inverses[0], image, HIGHEST)
                basis[0:K, BS:] = image
                following = image + known
            elif step == 1:
                following = image + known
            else:
                following = dot(inverses[step - 1], image + known, HIGHEST)
            sent(step)
            rounded = following.astype(BF16)
            after = step + 1
            raw_x[g, K * after : K * after + K, :] = following
            if after < ITERS:
                cols_x[after][r] = rounded
                rows_x[after][g] = rounded
                mine = rows_x[after].at[g]
                for dy in (2, 1, 3):
                    remote(
                        mine,
                        mine,
                        rows_send,
                        rows_recv.at[after % 2],
                        lax.rem(g + dy, GRP),
                        r,
                    ).start()
                send_cols(after)
            else:
                send_last()
                send_raw(after)

        def ahead(step=step, coef=coef, gram=gram, image=image):
            at = K * step
            if step > 0:
                coef, gram = scaled(step, coef, gram)
                normalise(step, coef, gram)
                both = jnp.concatenate([raw_x[g, at : at + K, :], image], axis=1)
                if step > 1:
                    both = dot(inverses[step - 1], both, HIGHEST)
                both = both - dot(coef, basis[0:at, :], HIGHEST)
                basis[at : at + K, :] = dot(inverses[step], both, HIGHEST)
                record(step, coef)
            if step == ITERS - 1:
                return None
            size = at + K
            in_blocks[0:size, :] = t_dot(
                trans[0:size, 0:size],
                basis[0:size, BS:] - SHIFT * basis[0:size, 0:BS],
                HIGHEST,
            )
            last = basis[at : at + K, 0:BS]
            return last if step == 0 else t_dot(inverses[step], last, HIGHEST)

    ahead()
    for i in range(GRP):
        old_rows[:, i * BS : (i + 1) * BS] = dot(trans[...], raw_x[i, 0 : K * ITERS, :], HIGHEST)
    receive_raw(ITERS)
    for i in range(GRP):
        next_ref[:, i * BS : (i + 1) * BS] = dot(
            inverses[ITERS - 1], raw_x[i, K * ITERS :, :], HIGHEST
        )
    with scope("wait_last"):
        spread_last()
    _, coef, gram = receive_dots(ITERS)
    coef, gram = scaled(ITERS, coef, gram)
    next_ref[...] = next_ref[...] - dot(coef, old_rows[...], HIGHEST)
    normalise(ITERS, coef, gram)
    with scope("final"):
        record(ITERS, coef)
        next_ref[...] = dot(inverses[ITERS], next_ref[...], HIGHEST)
    await_send(last.at[pl.ds(0, CHIPS - 1)], last_send, last_recv)
    await_send(start_gram.at[0], pair_gram_send, pair_gram_recv)
    await_send(start_grams.at[pl.ds(0, CHIPS - 1)], gram_send, gram_recv)
    await_send(dots.at[ITERS, pl.ds(0, 7)], dots_send, dots_recv.at[0])


def write_out(*refs):
    inputs, outputs, sems = refs[:3], refs[3:6], refs[6]
    copies = [pltpu.make_async_copy(inputs[i], outputs[i], sems.at[i]) for i in (2, 0, 1)]
    for copy in copies:
        copy.start()
    for copy in copies:
        copy.wait()


def per_device(tiles, tile_rows, tile_cols, live_tiles, dual_shift, start_block):
    hbm = pl.BlockSpec(memory_space=pltpu.HBM)
    vmem = pl.BlockSpec(memory_space=pltpu.VMEM)
    in_hbm = functools.partial(pltpu.with_memory_space_constraint, memory_space=pltpu.HBM)
    dma = pltpu.SemaphoreType.DMA
    steps = ITERS + 1
    out = pl.pallas_call(
        kernel,
        out_shape=(
            pltpu.VMEM((ITERS, K, ITERS * K), F32),
            pltpu.VMEM((ITERS, K, K), F32),
            pltpu.VMEM((K, GRP * BS), F32),
        ),
        in_specs=[hbm] * 6,
        out_specs=(vmem, vmem, vmem),
        scratch_shapes=[
            pltpu.SMEM((1, 1, TILES), jnp.int32),
            pltpu.SMEM((1, 1, TILES), jnp.int32),
            pltpu.SMEM((1, 1), jnp.int32),
            pltpu.VMEM((1, GRP * BS), F32),
            pltpu.VMEM((K, K), F32),
            pltpu.VMEM((2, 8, 128), F32),
            pltpu.VMEM((CHIPS, 8, 128), F32),
            pltpu.VMEM((1, GRP * ROW), jnp.int32),
            pltpu.SMEM((1, GRP * ROW), jnp.int32),
            pltpu.VMEM((K, GRP * BS), F32),
            pltpu.VMEM((TILES, BS, BS), BF16),
            pltpu.VMEM((TILES, BS, BS), BF16),
            *[pltpu.VMEM((ROW, height(step), BS), BF16) for step in range(ITERS)],
            *[pltpu.VMEM((GRP, height(step), BS), BF16) for step in range(ITERS)],
            pltpu.VMEM((GRP, K * steps, BS), F32),
            pltpu.VMEM((K * ITERS, 2 * BS), F32),
            pltpu.VMEM((K * ITERS, BS), F32),
            pltpu.VMEM((K * ITERS, GRP * BS), F32),
            pltpu.VMEM((K * ITERS, K * ITERS), F32),
            pltpu.VMEM((TILES + 1, K, BS), F32),
            pltpu.VMEM((ITERS, CHIPS, K, BS), BF16),
            pltpu.VMEM((ITERS, CHIPS, K, BS), BF16),
            pltpu.VMEM((ITERS, CHIPS, K, BS), BF16),
            pltpu.VMEM((ITERS, CHIPS, K, BS), BF16),
            pltpu.VMEM((CHIPS, K, BS), F32),
            pltpu.VMEM((K, BS), F32),
            pltpu.VMEM((ITERS, GRP, K, BS), BF16),
            pltpu.VMEM((ITERS, GRP, K, BS), BF16),
            pltpu.VMEM((steps, 2 * GRP, K + 8, 128), F32),
            pltpu.VMEM((CHIPS, K + 8, 128), F32),
            dma((5,)),
            dma,
            dma,
            dma,
            dma,
            dma,
            dma,
            dma,
            dma,
            dma,
            dma((2, len(WAVES))),
            *[dma, dma((2,))] * 7,
        ],
        compiler_params=pltpu.CompilerParams(
            collective_id=0, has_side_effects=True, vmem_limit_bytes=48 * 1024 * 1024
        ),
        name="lanczos",
    )(
        in_hbm(tile_rows),
        in_hbm(tile_cols),
        live_tiles,
        *[
            in_hbm(a)
            for a in (
                tiles.reshape(TILES, BS, BS),
                start_block,
                dual_shift.reshape(1, GRP * BS),
            )
        ]
    )
    return pl.pallas_call(
        write_out,
        out_shape=tuple(jax.ShapeDtypeStruct(a.shape, a.dtype) for a in out),
        in_specs=[vmem] * 3,
        out_specs=(hbm, hbm, hbm),
        scratch_shapes=[dma((3,))],
        compiler_params=pltpu.CompilerParams(vmem_limit_bytes=1024 * 1024),
        name="write_out",
    )(*[pltpu.with_memory_space_constraint(a, pltpu.VMEM) for a in out])


def solution(mesh):
    in_specs = (
        P("grp", "row", None, None, None),
        P("grp", "row", None),
        P("grp", "row", None),
        P("grp", "row"),
        P("row"),
        P(None, "row"),
    )
    out_specs = (P(), P(), P(None, "row"))
    return jax.shard_map(
        per_device, mesh=mesh, in_specs=in_specs, out_specs=out_specs, check_vma=False
    )
```

profile of v0, /device:TPU:1, one launch (start us, length us, event | category | flops | bytes accessed | tf_op | source)
XLA Modules:
  0.0 72.6 jit_solution(17355805370492241736)
XLA Ops:
  1.3 70.4 %lanczos.1 = (f32[4,32,128]{2,1,0:T(8,128)S(1)}, f32[4,32,32]{2,1,0:T(8,128)S(1)}, f32[32,1024]{1,0:T(8,128)S(1)}) custom-call(s32[1,1,32]{2,1,0:T(1,128)} %rows_hbm.1, s32[1,1,32]{2,1,0:T(1,128)} %cols_hbm.1, s32[1,1]{1,0:T(1,128)S(6)} %copy.9.live_hbm, bf16[32,256,256]{2,1,0:T(8,128)(2,1)} %bitcast.2, f32[32,1024]{1,0:T(8,128)} %start_hbm.1, f32[1,1024]{1,0:T(1,128)} %bitcast.3), custom_call_target="tpu_custom_call" | custom-call | tf_op jit(solution)/shard_map/lanczos/pallas_call | solution.py:680
  71.7 0.7 write_out.1
where the time goes:
time: 72.7 us; the launch traced here: 72.6 us
  Pallas kernels  71.1 us (98%)
  between operations  1.45 us (2%)
    pallas_call x1, Pallas kernels, per_device(): pl.pallas_call(kernel, out_shape=(pltpu.VMEM((ITERS, K, ITERS * K), F32),...  70.4 us

commit v1 on v0

--- a/solution.py
+++ b/solution.py
@@ -49,7 +49,7 @@
 
 
 def dots_height(step):
-    return K if step < ITERS else K + 8
+    return {1: K // 2, ITERS: K + 8}.get(step, K)
 
 
 def dot(left, right, precision=None):
@@ -288,7 +288,7 @@
         await_send(direct_in.at[step, pl.ds(0, 3)], direct_send, direct_recv.at[0])
         if step > 0:
             await_send(rows_x[step].at[pl.ds(0, 3)], rows_send, rows_recv.at[0])
-            await_send(dots.at[step, pl.ds(0, 7), pl.ds(0, K)], dots_send, dots_recv.at[0])
+            await_send(dots.at[step, pl.ds(0, 7), pl.ds(0, dots_height(step))], dots_send, dots_recv.at[0])
 
     def send_raw(step):
         if step > 1:
@@ -410,7 +410,11 @@
             totals[p % 4] = totals[p % 4] + dot_t(cols_x[step][owner], so_far)
         total = (totals[0] + totals[1]) + (totals[2] + totals[3])
         here = g * 2 + core
-        dots[step, here, 0:K, 0:width] = total
+        if step == 1:
+            dots[1, here, 0 : K // 2, 0:width] = total[: K // 2]
+            dots[1, here, 0 : K // 2, width:] = total[K // 2 :]
+        else:
+            dots[step, here, 0:K, 0:width] = total
         spread_dots(step)
 
     def spread_dots(step):
@@ -428,8 +432,9 @@
 
     def send_last():
         block = raw_x[g, K * ITERS :, :]
-        last[chip, 0:K, :] = dot_t(block, raw_x[g, 0 : K * ITERS, :], HIGHEST)
-        gram = dot_t(block, block, HIGHEST)
+        total = dot_t(block, raw_x[g], HIGHEST)
+        last[chip, 0:K, :] = total[:, 0 : K * ITERS]
+        gram = total[:, K * ITERS :]
         for i in range(4):
             last[chip, K:, i * K : (i + 1) * K] = gram[8 * i : 8 * i + 8]
         mine = last.at[chip]
@@ -454,6 +459,8 @@
         total = dots[step, 0, 0 : dots_height(step)]
         for i in range(1, 2 * GRP):
             total = total + dots[step, i, 0 : dots_height(step)]
+        if step == 1:
+            total = jnp.concatenate([total[:, : 2 * K], total[:, 2 * K :]], axis=0)
         if step < ITERS:
             gram = total[:, K * step : K + K * step]
         else:
@@ -462,12 +469,15 @@
         coef = dot_t(products_before, trans[0 : K * step, 0 : K * step], HIGHEST)
         return products_before, coef, gram - dot_t(coef, coef, HIGHEST)
 
+    def settle(gram):
+        gram_ref[...] = gram
+        return gram_ref[...]
+
     def scaled(step, coef, gram):
         if step > 1:
             coef = dot(inverses[step - 1], coef, HIGHEST)
             gram = dot_t(dot(inverses[step - 1], gram, HIGHEST), inverses[step - 1], HIGHEST)
-        gram_ref[...] = gram
-        return coef, gram_ref[...]
+        return coef, settle(gram)
 
     def normalise(step, coef, gram):
         with phase("cholesky"):
@@ -571,6 +581,7 @@
                 known = known - dot(before, in_blocks[0 : K * step, :], HIGHEST)
                 known = known - dot(gram, newest, HIGHEST)
 
+        sent(step)
         with scope("wait_direct"):
             await_recv(
                 direct_in.at[step, pl.ds(0, 3)], direct_send, direct_recv.at[step % 2]
@@ -595,7 +606,6 @@
                 following = image + known
             else:
                 following = dot(inverses[step - 1], image + known, HIGHEST)
-            sent(step)
             rounded = following.astype(BF16)
             after = step + 1
             raw_x[g, K * after : K * after + K, :] = following
@@ -643,19 +653,20 @@
     for i in range(GRP):
         old_rows[:, i * BS : (i + 1) * BS] = dot(trans[...], raw_x[i, 0 : K * ITERS, :], HIGHEST)
     receive_raw(ITERS)
-    for i in range(GRP):
-        next_ref[:, i * BS : (i + 1) * BS] = dot(
-            inverses[ITERS - 1], raw_x[i, K * ITERS :, :], HIGHEST
-        )
     with scope("wait_last"):
         spread_last()
     _, coef, gram = receive_dots(ITERS)
-    coef, gram = scaled(ITERS, coef, gram)
-    next_ref[...] = next_ref[...] - dot(coef, old_rows[...], HIGHEST)
-    normalise(ITERS, coef, gram)
+    gram = settle(gram)
+    for i in range(GRP):
+        here = slice(i * BS, (i + 1) * BS)
+        next_ref[:, here] = raw_x[i, K * ITERS :, :] - dot(coef, old_rows[:, here], HIGHEST)
+    with scope("cholesky"):
+        upper, inverse = cholesky(gram)
     with scope("final"):
-        record(ITERS, coef)
-        next_ref[...] = dot(inverses[ITERS], next_ref[...], HIGHEST)
+        next_ref[...] = dot(inverse, next_ref[...], HIGHEST)
+        fact_ref[ITERS - 1] = dot_t(inverses[ITERS - 1], upper, HIGHEST)
+        record(ITERS, dot(inverses[ITERS - 1], coef, HIGHEST))
+
     await_send(last.at[pl.ds(0, CHIPS - 1)], last_send, last_recv)
     await_send(start_gram.at[0], pair_gram_send, pair_gram_recv)
     await_send(start_grams.at[pl.ds(0, CHIPS - 1)], gram_send, gram_recv)

time: 72.7 us -> 72.5 us (level)
  no operation moved by 1% of the time
where the time goes in v1:
time: 72.5 us; the launch traced here: 72.4 us
  Pallas kernels  71 us (98%)
  between operations  1.45 us (2%)
    pallas_call x1, Pallas kernels, per_device(): pl.pallas_call(kernel, out_shape=(pltpu.VMEM((ITERS, K, ITERS * K), F32),...  70.3 us

profile of v1, /device:TPU:1, one launch (start us, length us, event | category | flops | bytes accessed | tf_op | source)
XLA Modules:
  0.0 72.4 jit_solution(1616707612114357023)
XLA Ops:
  1.3 70.3 %lanczos.1 = (f32[4,32,128]{2,1,0:T(8,128)S(1)}, f32[4,32,32]{2,1,0:T(8,128)S(1)}, f32[32,1024]{1,0:T(8,128)S(1)}) custom-call(s32[1,1,32]{2,1,0:T(1,128)} %rows_hbm.1, s32[1,1,32]{2,1,0:T(1,128)} %cols_hbm.1, s32[1,1]{1,0:T(1,128)S(6)} %copy.9.live_hbm, bf16[32,256,256]{2,1,0:T(8,128)(2,1)} %bitcast.2, f32[32,1024]{1,0:T(8,128)} %start_hbm.1, f32[1,1024]{1,0:T(1,128)} %bitcast.3), custom_call_target="tpu_custom_call" | custom-call | tf_op jit(solution)/shard_map/lanczos/pallas_call | solution.py:691
  71.5 0.7 write_out.1

commit v2 on v1

--- a/solution.py
+++ b/solution.py
@@ -21,7 +21,7 @@
 CHIPS = ROW // 2
 SIDE = 4
 TILES = 32
-WAVES = (5, 5, 3, 2)
+WAVES = (4, 3, 2, 2, 2, 1, 1)
 PARTS = 4
 SHIFT = -1.0
 

time: 72.5 us -> 72.5 us (level)
  no operation moved by 1% of the time
where the time goes in v2:
time: 72.5 us; the launch traced here: 72.4 us
  Pallas kernels  71 us (98%)
  between operations  1.45 us (2%)
    pallas_call x1, Pallas kernels, per_device(): pl.pallas_call(kernel, out_shape=(pltpu.VMEM((ITERS, K, ITERS * K), F32),...  70.2 us

profile of v2, /device:TPU:1, one launch (start us, length us, event | category | flops | bytes accessed | tf_op | source)
XLA Modules:
  0.0 72.4 jit_solution(9485815061359349963)
XLA Ops:
  1.3 70.2 %lanczos.1 = (f32[4,32,128]{2,1,0:T(8,128)S(1)}, f32[4,32,32]{2,1,0:T(8,128)S(1)}, f32[32,1024]{1,0:T(8,128)S(1)}) custom-call(s32[1,1,32]{2,1,0:T(1,128)} %rows_hbm.1, s32[1,1,32]{2,1,0:T(1,128)} %cols_hbm.1, s32[1,1]{1,0:T(1,128)S(6)} %copy.9.live_hbm, bf16[32,256,256]{2,1,0:T(8,128)(2,1)} %bitcast.2, f32[32,1024]{1,0:T(8,128)} %start_hbm.1, f32[1,1024]{1,0:T(1,128)} %bitcast.3), custom_call_target="tpu_custom_call" | custom-call | tf_op jit(solution)/shard_map/lanczos/pallas_call | solution.py:691
  71.5 0.7 write_out.1
